TPU v7x, 32 devices: a whole 2x2x4 slice. The times are simulated.
32 devices in a mesh: seq: 16 (over z, y, x), blk: 2 (over core).
Axes of the slice: x: 2, y: 2, z: 4, core: 2. Of those that a mesh axis runs over, the one named last changes fastest.
Arguments:
- query: bfloat16 [2048, 5120], P(('blk', 'seq')), may hold values from -139 to 139
- keys: bfloat16 [2048, 5120], P(('blk', 'seq')), may hold values from -4.5 to 4.5
- values: bfloat16 [2048, 5120], P(('blk', 'seq')), may hold values from -6 to 6
Outputs:
- attended: bfloat16 [2048, 5120], P(('blk', 'seq'))
All inputs are finite; a program needn't handle non-finite values.
Results may differ from a plain program's by a relative error of at most 0.008.
Values may be sent and summed in bfloat16 or wider, within the bound.
No kernel may reach another device: no remote copies, remote signals or barrier semaphores. Data moves between devices by JAX's collectives and lax.ppermute only.
A program may use at most 64 MiB of HBM per device.

v0:
```python
import jax
import jax.numpy as jnp
from jax import lax
from jax.sharding import PartitionSpec as P

HEADS = 40


def partner(value, axis, bit):
    mask = 2**bit
    pairs = [(source, source ^ mask) for source in range(lax.axis_size(axis))]
    return lax.ppermute(value, axis, pairs)


def partial_block(q_rows, k_tile, v_tile):
    scores = lax.dot_general(
        q_rows, k_tile, (((1,), (1,)), ((), ())), preferred_element_type=jnp.float32
    ) * q_rows.shape[1] ** (-0.5)
    peak = jnp.max(scores, axis=1)
    expo = jnp.exp(scores - peak[:, None])
    totals = jnp.sum(expo, axis=1)
    summed = jnp.dot(expo.astype(jnp.bfloat16), v_tile, preferred_element_type=jnp.float32)
    return (peak, totals, summed)


def combine_parts(left, right):
    peak = jnp.maximum(left[0], right[0])
    scale_left = jnp.exp(left[0] - peak)
    scale_right = jnp.exp(right[0] - peak)
    totals = scale_left * left[1] + scale_right * right[1]
    summed = scale_left[:, None] * left[2] + scale_right[:, None] * right[2]
    return (peak, totals, summed)


def attend_rows(q_rows, first_k, first_v, second_k, second_v):
    state = partial_block(q_rows, first_k, first_v)
    state = combine_parts(state, partial_block(q_rows, second_k, second_v))
    return (state[2] / state[1][:, None]).astype(jnp.bfloat16)


def attend_item(args):
    q_head, first_k, first_v, second_k, second_v = args
    length, width = q_head.shape
    rows = min(512, length)

    def block(q_rows):
        return attend_rows(q_rows, first_k, first_v, second_k, second_v)

    return lax.map(block, q_head.reshape(length // rows, rows, width)).reshape(length, width)


def items_first(array):
    return jnp.transpose(array.reshape(array.shape[0], array.shape[2], array.shape[3]), (1, 0, 2))


def attend_items(pieces):
    q_group, k_group, v_group = pieces
    q_heads = items_first(q_group)
    k_heads = items_first(k_group)
    v_heads = items_first(v_group)
    stacked = jnp.stack([k_heads, v_heads])
    other = partner(stacked, "blk", 0)
    tiles = (q_heads, k_heads, v_heads, other[0], other[1])
    outcome = lax.map(attend_item, tiles)
    count, length, width = outcome.shape
    outcome = jnp.transpose(outcome, (1, 0, 2)).reshape(length, 1, count, width)
    return lax.all_to_all(outcome, "seq", split_axis=0, concat_axis=1, tiled=True)


def on_device(query, keys, values):
    groups = lax.axis_size("seq")
    width = query.shape[1] // HEADS
    tok_rows = query.shape[0]
    key_source, value_source = (keys, values)
    per_dev = (HEADS + groups - 1) // groups
    slots_all = per_dev * groups

    def split_heads(array):
        count_rows = array.shape[0]
        shaped = array.reshape(count_rows, HEADS, width)
        shaped = jnp.pad(shaped, ((0, 0), (0, slots_all - HEADS), (0, 0)))
        return shaped.reshape(count_rows, groups, per_dev, width)

    result = attend_items(
        (
            lax.all_to_all(split_heads(query), "seq", split_axis=1, concat_axis=0, tiled=True),
            lax.all_to_all(split_heads(key_source), "seq", split_axis=1, concat_axis=0, tiled=True),
            lax.all_to_all(
                split_heads(value_source), "seq", split_axis=1, concat_axis=0, tiled=True
            ),
        )
    )
    result = result.reshape(tok_rows, slots_all, width)[:, :HEADS]
    return result.reshape(tok_rows, HEADS * width)


def solution(mesh):
    placed = (P(("blk", "seq"), None), P(("blk", "seq"), None), P(("blk", "seq"), None))
    return jax.shard_map(
        on_device, mesh=mesh, in_specs=placed, out_specs=P(("blk", "seq"), None), check_vma=False
    )
```

profile of v0, /device:TPU:0, one launch (start us, length us, event | category | flops | bytes accessed | tf_op | source)
XLA Modules:
  0.0 155.3 jit_solution(6471587082868300585)
XLA Ops:
  0.0 1.1 copy-done
  1.3 1.0 pad.11.clone
  2.2 8.3 %all-to-all-start.1 = ((bf16[64,16,3,128]{3,0,2,1:T(8,128)(2,1)}), bf16[64,16,3,128]{3,0,2,1:T(8,128)(2,1)S(1)}, u32[]{:S(2)}, u32[]{:S(2)}) async-start(bf16[64,16,3,128]{3,0,2,1:T(8,128)(2,1)} %bitcast.13), calls=%async_computation.1 | async-start | bytes 1572864 | tf_op jit(solution)/shard_map/all_to_all | solution.py:87
  10.8 1.0 pad.12.clone
  11.8 18.5 %all-to-all-done.1 = bf16[64,16,3,128]{3,0,2,1:T(8,128)(2,1)S(1)} async-done(((bf16[64,16,3,128]{3,0,2,1:T(8,128)(2,1)}), bf16[64,16,3,128]{3,0,2,1:T(8,128)(2,1)S(1)}, u32[]{:S(2)}, u32[]{:S(2)}) %all-to-all-start.1) | async-done | bytes 786464 | tf_op jit(solution)/shard_map/all_to_all | solution.py:87
  30.3 5.0 %all-to-all-start.2 = ((bf16[64,16,3,128]{3,0,2,1:T(8,128)(2,1)}), bf16[64,16,3,128]{3,0,2,1:T(8,128)(2,1)S(1)}, u32[]{:S(2)}, u32[]{:S(2)}) async-start(bf16[64,16,3,128]{3,0,2,1:T(8,128)(2,1)} %bitcast.18), calls=%async_computation.2 | async-start | bytes 1572864 | tf_op jit(solution)/shard_map/all_to_all | solution.py:88
  35.3 18.6 %all-to-all-done.2 = bf16[64,16,3,128]{3,0,2,1:T(8,128)(2,1)S(1)} async-done(((bf16[64,16,3,128]{3,0,2,1:T(8,128)(2,1)}), bf16[64,16,3,128]{3,0,2,1:T(8,128)(2,1)S(1)}, u32[]{:S(2)}, u32[]{:S(2)}) %all-to-all-start.2) | async-done | bytes 786464 | tf_op jit(solution)/shard_map/all_to_all | solution.py:88
  54.8 1.3 copy.18
  56.0 1.3 pad_maximum_fusion
  57.5 1.0 pad.10.clone
  58.5 5.0 %all-to-all-start = ((bf16[64,16,3,128]{3,0,2,1:T(8,128)(2,1)}), bf16[64,16,3,128]{3,0,2,1:T(8,128)(2,1)S(1)}, u32[]{:S(2)}, u32[]{:S(2)}) async-start(bf16[64,16,3,128]{3,0,2,1:T(8,128)(2,1)} %bitcast.121), calls=%async_computation | async-start | bytes 1572864 | tf_op jit(solution)/shard_map/all_to_all | solution.py:86
  63.4 20.1 %all-to-all-done = bf16[64,16,3,128]{3,0,2,1:T(8,128)(2,1)S(1)} async-done(((bf16[64,16,3,128]{3,0,2,1:T(8,128)(2,1)}), bf16[64,16,3,128]{3,0,2,1:T(8,128)(2,1)S(1)}, u32[]{:S(2)}, u32[]{:S(2)}) %all-to-all-start) | async-done | bytes 786464 | tf_op jit(solution)/shard_map/all_to_all | solution.py:86
  84.5 2.6 %slice_bitcast_fusion = (bf16[3,1024,128]{2,1,0:T(8,128)(2,1)}, bf16[3,1024,128]{2,1,0:T(8,128)(2,1)}) fusion(bf16[2,3,1024,128]{3,2,1,0:T(8,128)(2,1)} %collective-permute-done), kind=kLoop, calls=%fused_computation.42 | loop fusion | bytes 3145728 | tf_op jit(solution)/shard_map/squeeze | solution.py:63
  87.1 34.5 %while.21 = (s32[]{:T(128)}, bf16[3,1024,128]{2,1,0:T(8,128)(2,1)}, bf16[3,1024,128]{2,1,0:T(8,128)(2,1)}, bf16[3,1024,128]{2,1,0:T(8,128)(2,1)S(1)}, bf16[3,102...) while((s32[]{:T(128)}, bf16[3,1024,128]{2,1,0:T(8,128)(2,1)}, ...), condition=%wide.region_7.8_spmd, body=%wide.region_0.7_spmd.sunk | while | flops 545588224 | bytes 18780980 | solution.py:64
  87.1 1.0 dynamic-slice_bitcast_fusion.6
  88.1 1.7 %dynamic-slice_bitcast_fusion.7 = (bf16[1024,128]{1,0:T(8,128)(2,1)}, bf16[1024,128]{1,0:T(8,128)(2,1)S(1)}) fusion(bf16[3,1024,128]{2,1,0:T(8,128)(2,1)} %get-tuple-element.302, s32[]{:T(128)} %get-tuple-element.286, bf16[3,1024,128]{2,1,0:T(8,128)(2,1)S(1)} %get-tuple-element.300), kind=kLoop, calls=%fused_computation.35.clone.1 | loop fusion | bytes 1048580 | tf_op jit(solution)/shard_map/while/body/jit(dynamic_index_in_dim)/squeeze | solution.py:64
  89.8 1.0 constant_dynamic-slice_fusion.2
  90.8 7.1 %while.22 = (s32[]{:T(128)}, bf16[2,512,128]{2,1,0:T(8,128)(2,1)S(1)}, bf16[2,512,128]{2,1,0:T(8,128)(2,1)S(1)}, bf16[1024,128]{1,0:T(8,128)(2,1)S(1)}, bf16[102...) while((s32[]{:T(128)}, ...), condition=%wide.region_6.6_spmd, body=%wide.region_1.5_spmd.sunk | while | flops 545588224 | bytes 15634557 | solution.py:49
  91.8 1.0 fusion.50
  95.4 1.0 fusion.50
  98.6 1.0 dynamic-slice_bitcast_fusion.6
  99.6 1.7 %dynamic-slice_bitcast_fusion.7 = (bf16[1024,128]{1,0:T(8,128)(2,1)}, bf16[1024,128]{1,0:T(8,128)(2,1)S(1)}) fusion(bf16[3,1024,128]{2,1,0:T(8,128)(2,1)} %get-tuple-element.302, s32[]{:T(128)} %get-tuple-element.286, bf16[3,1024,128]{2,1,0:T(8,128)(2,1)S(1)} %get-tuple-element.300), kind=kLoop, calls=%fused_computation.35.clone.1 | loop fusion | bytes 1048580 | tf_op jit(solution)/shard_map/while/body/jit(dynamic_index_in_dim)/squeeze | solution.py:64
  101.3 1.0 constant_dynamic-slice_fusion.2
  102.3 7.1 %while.22 = (s32[]{:T(128)}, bf16[2,512,128]{2,1,0:T(8,128)(2,1)S(1)}, bf16[2,512,128]{2,1,0:T(8,128)(2,1)S(1)}, bf16[1024,128]{1,0:T(8,128)(2,1)S(1)}, bf16[102...) while((s32[]{:T(128)}, ...), condition=%wide.region_6.6_spmd, body=%wide.region_1.5_spmd.sunk | while | flops 545588224 | bytes 15634557 | solution.py:49
  103.3 1.0 fusion.50
  110.1 1.0 dynamic-slice_bitcast_fusion.6
  111.1 1.7 %dynamic-slice_bitcast_fusion.7 = (bf16[1024,128]{1,0:T(8,128)(2,1)}, bf16[1024,128]{1,0:T(8,128)(2,1)S(1)}) fusion(bf16[3,1024,128]{2,1,0:T(8,128)(2,1)} %get-tuple-element.302, s32[]{:T(128)} %get-tuple-element.286, bf16[3,1024,128]{2,1,0:T(8,128)(2,1)S(1)} %get-tuple-element.300), kind=kLoop, calls=%fused_computation.35.clone.1 | loop fusion | bytes 1048580 | tf_op jit(solution)/shard_map/while/body/jit(dynamic_index_in_dim)/squeeze | solution.py:64
  112.8 1.0 constant_dynamic-slice_fusion.2
  113.8 7.1 %while.22 = (s32[]{:T(128)}, bf16[2,512,128]{2,1,0:T(8,128)(2,1)S(1)}, bf16[2,512,128]{2,1,0:T(8,128)(2,1)S(1)}, bf16[1024,128]{1,0:T(8,128)(2,1)S(1)}, bf16[102...) while((s32[]{:T(128)}, ...), condition=%wide.region_6.6_spmd, body=%wide.region_1.5_spmd.sunk | while | flops 545588224 | bytes 15634557 | solution.py:49
  114.8 1.0 fusion.50
  121.6 1.8 %copy.35 = bf16[3,1024,128]{2,0,1:T(4,128)(2,1)S(1)} copy(bf16[3,1024,128]{2,1,0:T(8,128)(2,1)} %get-tuple-element.79) | data formatting | bytes 1572864 | tf_op jit(solution)/shard_map/while | solution.py:64
  123.4 30.8 %all_to_all.60 = bf16[1024,1,3,128]{3,2,1,0:T(4,128)(2,1)S(1)} all-to-all(bf16[1024,1,3,128]{3,2,1,0:T(4,128)(2,1)S(1)} %bitcast.116), channel_id=1, replica_groups=mesh['seq'=16,'blk'=2] {'seq'}, dimensions={0} | all-to-all | bytes 1572864 | tf_op jit(solution)/shard_map/all_to_all | solution.py:67
  (68 shorter events, 23.0 us)
Async XLA Ops:
  0.0 1.1 copy-start
  0.0 10.6 %copy-start.3 = (bf16[64,5120]{1,0:T(8,128)(2,1)S(1)}, bf16[64,5120]{1,0:T(8,128)(2,1)}, u32[]{:S(2)}) copy-start(bf16[64,5120]{1,0:T(8,128)(2,1)} %param.9) | copy-start | bytes 1966084
  2.2 28.0 %all-to-all-start.1 = ((bf16[64,16,3,128]{3,0,2,1:T(8,128)(2,1)}), bf16[64,16,3,128]{3,0,2,1:T(8,128)(2,1)S(1)}, u32[]{:S(2)}, u32[]{:S(2)}) async-start(bf16[64,16,3,128]{3,0,2,1:T(8,128)(2,1)} %bitcast.13), calls=%async_computation.1 | async-start | bytes 1572864 | tf_op jit(solution)/shard_map/all_to_all | solution.py:87
  30.3 23.6 %all-to-all-start.2 = ((bf16[64,16,3,128]{3,0,2,1:T(8,128)(2,1)}), bf16[64,16,3,128]{3,0,2,1:T(8,128)(2,1)S(1)}, u32[]{:S(2)}, u32[]{:S(2)}) async-start(bf16[64,16,3,128]{3,0,2,1:T(8,128)(2,1)} %bitcast.18), calls=%async_computation.2 | async-start | bytes 1572864 | tf_op jit(solution)/shard_map/all_to_all | solution.py:88
  53.9 0.9 copy-start.2
  54.8 2.6 %copy-start.4 = (bf16[64,5120]{1,0:T(8,128)(2,1)S(1)}, bf16[64,5120]{1,0:T(8,128)(2,1)}, u32[]{:S(2)}) copy-start(bf16[64,5120]{1,0:T(8,128)(2,1)} %param.7) | copy-start | bytes 1966084
  57.3 27.2 %collective-permute-start = (bf16[2,3,1024,128]{3,2,1,0:T(8,128)(2,1)}, bf16[2,3,1024,128]{3,2,1,0:T(8,128)(2,1)}, u32[]{:S(2)}, u32[]{:S(2)}) collective-permute-start(bf16[2,3,1024,128]{3,2,1,0:T(8,128)(2,1)} %pad_maximum_fusion), channel_id=1, source_target_pairs={{0,1},{1,0},{2,3},{3,2},{4,5},{5,4},{6,7},{7,6},{8,9},{9,8},{10,11... | collective-permute-start | bytes 4718600 | tf_op jit(solution)/shard_map/ppermute | solution.py:12
  58.5 25.1 %all-to-all-start = ((bf16[64,16,3,128]{3,0,2,1:T(8,128)(2,1)}), bf16[64,16,3,128]{3,0,2,1:T(8,128)(2,1)S(1)}, u32[]{:S(2)}, u32[]{:S(2)}) async-start(bf16[64,16,3,128]{3,0,2,1:T(8,128)(2,1)} %bitcast.121), calls=%async_computation | async-start | bytes 1572864 | tf_op jit(solution)/shard_map/all_to_all | solution.py:86
  92.8 1.0 copy-start.1
  96.3 1.0 copy-start.1
  104.3 1.0 copy-start.1
  107.8 1.0 copy-start.1
  115.8 1.0 copy-start.1
  119.3 1.0 copy-start.1
where the time goes:
time: 156 us; the launch traced here: 155 us
  waiting for transfers between devices  57.1 us (37%)
  blocking collectives  30.8 us (20%)
  local copies, waits for them, and re-layouts  28.7 us (18%)
  starting transfers between devices  18.2 us (12%)
  matrix products  12.9 us (8%)
  other arithmetic  7.11 us (5%)
    all_to_all x1, blocking collectives, attend_items(): lax.all_to_all(outcome, 'seq', split_axis=0, concat_axis=1, tiled=True)  30.8 us
    all_to_all x1, waiting for transfers between devices, on_device(): lax.all_to_all(split_heads(query), 'seq', split_axis=1, concat_axis=0, ti...  20.1 us
    all_to_all x1, waiting for transfers between devices, on_device(): lax.all_to_all(split_heads(value_source), 'seq', split_axis=1, concat_axi...  18.6 us
    all_to_all x1, waiting for transfers between devices, on_device(): lax.all_to_all(split_heads(key_source), 'seq', split_axis=1, concat_axis=...  18.5 us
    all_to_all x1, starting transfers between devices, on_device(): lax.all_to_all(split_heads(key_source), 'seq', split_axis=1, concat_axis=...  8.34 us
    squeeze x6, local copies, waits for them, and re-layouts, attend_items(): outcome = lax.map(attend_item, tiles)  8.03 us
    dot_general x12, matrix products, partial_block(): jnp.dot(expo.astype(jnp.bfloat16), v_tile, preferred_element_type=jnp.flo...  6.67 us
    dot_general x12, matrix products, partial_block(): lax.dot_general(q_rows, k_tile, (((1,), (1,)), ((), ())), preferred_eleme...  6.23 us
  transfers between devices with their start and end apart: 4, of which 3 were waited for; matrix products, arithmetic and copies ran while one was open for 2% of the time, Pallas kernels for 0%

commit v1 on v0

v1 whole, which is shorter than its diff:
```python
import functools
import math

import jax
import jax.numpy as jnp
from jax import lax
from jax.experimental import pallas as pl
from jax.sharding import PartitionSpec as P

HEADS = 40
LOG2E = 1.4426950408889634
KEY_TILE = 1024


def partner(value, axis, mask):
    pairs = [(source, source ^ mask) for source in range(lax.axis_size(axis))]
    return lax.ppermute(value, axis, pairs)


def attention_kernel(*refs):
    q_ref, o_ref = refs[0], refs[-1]
    kv_refs = refs[1:-1]
    width = q_ref.shape[-1]
    q_rows = q_ref[...].reshape(-1, width)
    factor = width ** (-0.5) * LOG2E
    peak = None
    for k_ref, v_ref in zip(kv_refs[0::2], kv_refs[1::2]):
        step = max(1, KEY_TILE // k_ref.shape[-2])
        for at in range(0, k_ref.shape[0], step):
            k_tile = k_ref[at : at + step].reshape(-1, width)
            v_tile = v_ref[at : at + step].reshape(-1, width)
            scores = lax.dot_general(
                q_rows, k_tile, (((1,), (1,)), ((), ())), preferred_element_type=jnp.float32
            )
            tile_peak = jnp.max(scores, axis=1, keepdims=True)
            if peak is None:
                peak = tile_peak
                expo = jnp.exp2((scores - peak) * factor)
                totals = jnp.sum(expo, axis=1, keepdims=True)
                summed = jnp.dot(
                    expo.astype(jnp.bfloat16), v_tile, preferred_element_type=jnp.float32
                )
            else:
                new_peak = jnp.maximum(peak, tile_peak)
                keep = jnp.exp2((peak - new_peak) * factor)
                peak = new_peak
                expo = jnp.exp2((scores - peak) * factor)
                totals = totals * keep + jnp.sum(expo, axis=1, keepdims=True)
                summed = summed * keep + jnp.dot(
                    expo.astype(jnp.bfloat16), v_tile, preferred_element_type=jnp.float32
                )
    o_ref[...] = (summed / totals).astype(jnp.bfloat16).reshape(o_ref.shape)


def attend(own, others):
    sources, _, count, rows, width = own.shape

    def item(array, index):
        return pl.BlockSpec(
            (array.shape[0], pl.squeezed, pl.squeezed, rows, width),
            lambda head: (0, index, head, 0, 0),
        )

    operands, specs = [own, own, own], [item(own, 0), item(own, 1), item(own, 2)]
    for other in others:
        base = other.shape[1] - 2
        operands += [other, other]
        specs += [item(other, base), item(other, base + 1)]
    return pl.pallas_call(
        attention_kernel,
        grid=(count,),
        in_specs=specs,
        out_specs=pl.BlockSpec(
            (sources, pl.squeezed, rows, width), lambda head: (0, head, 0, 0)
        ),
        out_shape=jax.ShapeDtypeStruct((sources, count, rows, width), jnp.bfloat16),
    )(*operands)


def on_device(query, keys, values):
    devices = lax.axis_size("seq")
    rows = query.shape[0]
    width = query.shape[1] // HEADS
    groups = math.gcd(HEADS, devices)
    members = devices // groups
    in_group = HEADS // groups
    whole = in_group // members
    shared = in_group - whole * members
    columns = [[g * members + m for g in range(groups)] for m in range(members)]

    def by_group(array):
        return array.reshape(rows, groups, in_group, width)

    arrays = [by_group(array) for array in (query, keys, values)]
    results = []
    if whole:
        own = jnp.stack(
            [
                array[:, :, : whole * members].reshape(rows, devices, whole, width)
                for array in arrays
            ]
        )
        own = jnp.transpose(own, (2, 0, 3, 1, 4))
        main = lax.all_to_all(own, "seq", split_axis=0, concat_axis=0, tiled=True)
    if shared:
        part = jnp.stack([array[:, :, whole * members :] for array in arrays])
        part = jnp.transpose(part, (2, 0, 3, 1, 4))
        part = lax.all_to_all(
            part, "seq", split_axis=0, concat_axis=0, tiled=True, axis_index_groups=columns
        )
    if whole:
        main_other = partner(main, "blk", 1)
        main_out = attend(main, [main_other])
    if shared:
        gathered = [part[:, 1:]]
        for step in range(1, members):
            pairs = [
                (g * members + m, g * members + (m + step) % members)
                for g in range(groups)
                for m in range(members)
            ]
            gathered.append(lax.ppermute(gathered[0], "seq", pairs))
        far = partner(jnp.stack(gathered), "blk", 1)
        part_out = attend(part, gathered[1:] + [far[i] for i in range(members)])
    if whole:
        back = lax.all_to_all(main_out, "seq", split_axis=0, concat_axis=0, tiled=True)
        back = back.reshape(groups, members, whole, rows, width)
        results.append(back.reshape(groups, members * whole, rows, width))
    if shared:
        results.append(
            lax.all_to_all(
                part_out, "seq", split_axis=0, concat_axis=0, tiled=True, axis_index_groups=columns
            )
        )
    result = jnp.concatenate(results, axis=1) if len(results) > 1 else results[0]
    return jnp.transpose(result, (2, 0, 1, 3)).reshape(rows, HEADS * width)


def solution(mesh):
    placed = (P(("blk", "seq"), None), P(("blk", "seq"), None), P(("blk", "seq"), None))
    return jax.shard_map(
        on_device, mesh=mesh, in_specs=placed, out_specs=P(("blk", "seq"), None), check_vma=False
    )
```

time: 156 us -> 121 us (0.78)
  blocking collectives: 30.8 us -> 0 us
  matrix products: 12.9 us -> 0 us
  local copies, waits for them, and re-layouts: 28.7 us -> 16.6 us
  Pallas kernels: 0 us -> 11.3 us
  starting transfers between devices: 18.2 us -> 28.2 us
  waiting for transfers between devices: 57.1 us -> 62.3 us
  other arithmetic: 7.11 us -> 1.98 us
    all_to_all x1 -> x0, blocking collectives: 30.8 us -> none  [attend_items(): lax.all_to_all(outcome, 'seq', split_axis=0, concat_axis=1, tiled=True)]
    dot_general x24 -> x0, matrix products: 12.9 us -> none  [the longest x12 6.67 us: partial_block(): jnp.dot(expo.astype(jnp.bfloat16), v_tile, preferred_element_type=jnp.flo...]
    pallas_call x0 -> x2, Pallas kernels: none -> 11.3 us  [attend(): pl.pallas_call(attention_kernel, grid=(count,), in_specs=specs, out_specs...]
    squeeze x7 -> x1, local copies, waits for them, and re-layouts: 10.7 us -> 0.84 us  [on_device(): part_out = attend(part, gathered[1:] + [far[i] for i in range(members)])]
    all_to_all x3 -> x4, starting transfers between devices: 18.2 us -> 27.1 us  [the longest x1 8.34 us: on_device(): main = lax.all_to_all(own, 'seq', split_axis=0, concat_axis=0, tiled=True)]
    reduce_sum x6 -> x0, other arithmetic: 5.74 us -> none  [partial_block(): totals = jnp.sum(expo, axis=1)]
    ppermute x0 -> x1, waiting for transfers between devices: none -> 5.43 us  [on_device(): gathered.append(lax.ppermute(gathered[0], 'seq', pairs))]
    slice x0 -> x6, local copies, waits for them, and re-layouts: none -> 5.25 us  [the longest x3 3.33 us: on_device(): part = jnp.stack([array[:, :, whole * members:] for array in arrays])]
  transfers between devices with their start and end apart: 4 -> 7, of which waited for: 3 -> 5; matrix products, arithmetic and copies ran while one was open for 2% -> 5% of each run, Pallas kernels for 0% -> 9%
where the time goes in v1:
time: 121 us
  waiting for transfers between devices  62.3 us (51%)
  starting transfers between devices  28.2 us (23%)
  local copies, waits for them, and re-layouts  16.6 us (14%)
  Pallas kernels  11.3 us (9%)
  other arithmetic  1.98 us (2%)
    all_to_all x1, waiting for transfers between devices, on_device(): main = lax.all_to_all(own, 'seq', split_axis=0, concat_axis=0, tiled=True)  29.8 us
    all_to_all x1, waiting for transfers between devices, on_device(): lax.all_to_all(main_out, 'seq', split_axis=0, concat_axis=0, tiled=True)  14.6 us
    pallas_call x2, Pallas kernels, attend(): pl.pallas_call(attention_kernel, grid=(count,), in_specs=specs, out_specs...  11.3 us
    all_to_all x1, waiting for transfers between devices, on_device(): lax.all_to_all(part, 'seq', split_axis=0, concat_axis=0, tiled=True, axis...  10.6 us
    all_to_all x1, starting transfers between devices, on_device(): main = lax.all_to_all(own, 'seq', split_axis=0, concat_axis=0, tiled=True)  8.34 us
    all_to_all x1, starting transfers between devices, on_device(): lax.all_to_all(part, 'seq', split_axis=0, concat_axis=0, tiled=True, axis...  7.53 us
    all_to_all x1, starting transfers between devices, on_device(): lax.all_to_all(main_out, 'seq', split_axis=0, concat_axis=0, tiled=True)  6.51 us
    ppermute x1, waiting for transfers between devices, on_device(): gathered.append(lax.ppermute(gathered[0], 'seq', pairs))  5.43 us
  transfers between devices with their start and end apart: 7, of which 5 were waited for; matrix products, arithmetic and copies ran while one was open for 5% of the time, Pallas kernels for 9%

profile of v1, /device:TPU:0, one launch (start us, length us, event | category | flops | bytes accessed | tf_op | source)
XLA Modules:
  0.0 120.7 jit_solution(8428344954867104243)
XLA Ops:
  0.0 1.9 %reshape.12 = bf16[64,8,5,128]{3,2,1,0:T(8,128)(2,1)S(1)} reshape(bf16[64,5120]{1,0:T(8,128)(2,1)} %param.3) | data formatting | bytes 1310720 | tf_op jit(solution)/shard_map/reshape | solution.py:92
  1.9 0.2 slice.36
  2.2 0.2 copy.87
  2.4 0.8 reshape.13
  3.2 0.2 slice.37
  3.4 1.0 copy.88
  4.4 0.3 copy-done.7
  4.7 1.8 %reshape.14 = bf16[64,8,5,128]{3,2,1,0:T(8,128)(2,1)} reshape(bf16[64,5120]{1,0:T(8,128)(2,1)S(1)} %copy-done.7) | data formatting | bytes 1310720 | tf_op jit(solution)/shard_map/reshape | solution.py:92
  6.5 1.5 %slice.38 = bf16[64,8,4,128]{3,2,1,0:T(4,128)(2,1)S(1)} slice(bf16[64,8,5,128]{3,2,1,0:T(8,128)(2,1)} %reshape.14), slice={[0:64], [0:8], [0:4], [0:128]} | slice | bytes 1048576 | tf_op jit(solution)/shard_map/slice | solution.py:99
  8.0 0.2 copy.89
  8.2 1.3 %maximum_bitcast_fusion = bf16[16,3,2,64,128]{4,3,2,1,0:T(8,128)(2,1)} fusion(bf16[1,64,16,2,128]{4,1,3,0,2:T(8,128)(2,1)S(1)} %copy.89, bf16[1,64,16,2,128]{4,1,3,0,2:T(8,128)(2,1)S(1)} %copy-done.5, bf16[1,64,16,2,128]{4,1,3,0,2:T(8,128)(2,1)S(1)} %copy.87), kind=kLoop, calls=%fused_computation | loop fusion | flops 1572864 | bytes 3145728 | tf_op jit(solution)/shard_map/transpose | solution.py:103
  9.6 8.3 %all-to-all-start = ((bf16[16,3,2,64,128]{4,3,2,1,0:T(8,128)(2,1)}), bf16[16,3,2,64,128]{4,3,2,1,0:T(8,128)(2,1)S(1)}, u32[]{:S(2)}, u32[]{:S(2)}) async-start(bf16[16,3,2,64,128]{4,3,2,1,0:T(8,128)(2,1)} %maximum_bitcast_fusion), calls=%async_computation | async-start | bytes 3145728 | tf_op jit(solution)/shard_map/all_to_all | solution.py:104
  17.9 0.3 slice.39
  18.2 1.5 %slice.40 = bf16[64,8,1,128]{3,2,1,0:T(2,128)(2,1)S(1)} slice(bf16[64,8,5,128]{3,2,1,0:T(8,128)(2,1)} %copy-done.3), slice={[0:64], [0:8], [4:5], [0:128]} | slice | bytes 262144 | tf_op jit(solution)/shard_map/slice | solution.py:106
  19.7 1.5 %slice.41 = bf16[64,8,1,128]{3,2,1,0:T(2,128)(2,1)S(1)} slice(bf16[64,8,5,128]{3,2,1,0:T(8,128)(2,1)} %reshape.14), slice={[0:64], [0:8], [4:5], [0:128]} | slice | bytes 262144 | tf_op jit(solution)/shard_map/slice | solution.py:106
  21.4 0.8 copy.90
  22.2 29.8 %all-to-all-done.refs_0_.refs_1_.refs_2_ = bf16[16,3,2,64,128]{4,3,2,1,0:T(8,128)(2,1)S(1)} async-done(((bf16[16,3,2,64,128]{4,3,2,1,0:T(8,128)(2,1)}), bf16[16,3,2,64,128]{4,3,2,1,0:T(8,128)(2,1)S(1)}, u32[]{:S(2)}, u32[]{:S(2)}) %all-to-all-start) | async-done | bytes 1572896 | tf_op jit(solution)/shard_map/all_to_all | solution.py:104
  52.0 7.5 %all-to-all-start.2 = ((bf16[8,3,1,64,128]{4,3,1,2,0:T(8,128)(2,1)}), bf16[8,3,1,64,128]{4,3,1,2,0:T(8,128)(2,1)S(1)}, u32[]{:S(2)}, u32[]{:S(2)}) async-start(bf16[8,3,1,64,128]{4,3,1,2,0:T(8,128)(2,1)} %copy.90), calls=%async_computation.2 | async-start | bytes 786432 | tf_op jit(solution)/shard_map/all_to_all | solution.py:108
  59.5 10.6 %all-to-all-done.2 = bf16[8,3,1,64,128]{4,3,1,2,0:T(8,128)(2,1)S(1)} async-done(((bf16[8,3,1,64,128]{4,3,1,2,0:T(8,128)(2,1)}), bf16[8,3,1,64,128]{4,3,1,2,0:T(8,128)(2,1)S(1)}, u32[]{:S(2)}, u32[]{:S(2)}) %all-to-all-start.2) | async-done | bytes 393248 | tf_op jit(solution)/shard_map/all_to_all | solution.py:108
  70.2 1.0 collective-permute-start.1
  71.2 5.4 %collective-permute-done.1 = bf16[8,2,1,64,128]{4,3,1,0,2:T(8,128)(2,1)S(1)} collective-permute-done((bf16[8,2,1,64,128]{4,3,1,0,2:T(8,128)(2,1)S(1)}, bf16[8,2,1,64,128]{4,3,1,0,2:T(8,128)(2,1)S(1)}, u32[]{:S(2)}, u32[]{:S(2)}) %collective-permute-start.1) | collective-permute-done | bytes 262176 | tf_op jit(solution)/shard_map/ppermute | solution.py:122
  76.8 1.9 %collective-permute-done.2 = bf16[2,8,2,1,64,128]{5,4,2,1,3,0:T(8,128)(2,1)S(1)} collective-permute-done((bf16[2,8,2,1,64,128]{5,4,2,1,3,0:T(8,128)(2,1)S(1)}, bf16[2,8,2,1,64,128]{5,4,2,1,3,0:T(8,128)(2,1)S(1)}, u32[]{:S(2)}, u32[]{:S(2)}) %collective-permute-start.2) | collective-permute-done | bytes 524320 | tf_op jit(solution)/shard_map/ppermute | solution.py:17
  78.7 0.8 slice_bitcast_fusion
  79.6 3.6 %shard_map.38 = bf16[8,1,64,128]{3,2,1,0:T(8,128)(2,1)} custom-call(bf16[8,3,1,64,128]{4,3,2,1,0:T(8,128)(2,1)} %bitcast.30, bf16[8,3,1,64,128]{4,3,2,1,0:T(8,128)(2,1)} %bitcast.31, bf16[8,3,1,64,128]{4,3,2,1,0:T(8,128)(2,1)} %bitcast.32, bf16[8,2,1,64,128]{4,3,2,1,0:T(8,128)(2,1)} %bitcast.34, bf16[8,2,1,64,128]{4,3,2,1,0:T(8,128)(2,1)} %bitcast.35, ...), custom_call_target="tpu_custom_call" | custom-call | tf_op jit(solution)/shard_map/pallas_call | solution.py:69
  83.2 4.8 %all-to-all-start.3 = ((bf16[8,1,64,128]{3,2,1,0:T(8,128)(2,1)}), bf16[8,1,64,128]{3,2,1,0:T(8,128)(2,1)S(1)}, u32[]{:S(2)}, u32[]{:S(2)}) async-start(bf16[8,1,64,128]{3,2,1,0:T(8,128)(2,1)} %shard_map.38), calls=%async_computation.3 | async-start | bytes 262144 | tf_op jit(solution)/shard_map/all_to_all | solution.py:131
  88.0 1.1 copy-done.2
  89.1 7.7 %shard_map.37 = bf16[16,2,64,128]{3,2,1,0:T(8,128)(2,1)} custom-call(bf16[16,3,2,64,128]{4,3,2,1,0:T(8,128)(2,1)} %copy-done, bf16[16,3,2,64,128]{4,3,2,1,0:T(8,128)(2,1)} %copy-done, bf16[16,3,2,64,128]{4,3,2,1,0:T(8,128)(2,1)} %copy-done, bf16[16,3,2,64,128]{4,3,2,1,0:T(8,128)(2,1)} %copy-done.2, bf16[16,3,2,64,128]{4,3,2,1,0:T(8,128)(2,1)} %copy-done.2), custom_call_target="tpu_custom_call" | custom-call | tf_op jit(solution)/shard_map/pallas_call | solution.py:69
  96.8 6.5 %all-to-all-start.1 = ((bf16[16,2,64,128]{3,2,1,0:T(8,128)(2,1)}), bf16[16,2,64,128]{3,2,1,0:T(8,128)(2,1)S(1)}, u32[]{:S(2)}, u32[]{:S(2)}) async-start(bf16[16,2,64,128]{3,2,1,0:T(8,128)(2,1)} %shard_map.37), calls=%async_computation.1 | async-start | bytes 1048576 | tf_op jit(solution)/shard_map/all_to_all | solution.py:126
  103.5 14.6 %all-to-all-done.1 = bf16[16,2,64,128]{3,2,1,0:T(8,128)(2,1)S(1)} async-done(((bf16[16,2,64,128]{3,2,1,0:T(8,128)(2,1)}), bf16[16,2,64,128]{3,2,1,0:T(8,128)(2,1)S(1)}, u32[]{:S(2)}, u32[]{:S(2)}) %all-to-all-start.1) | async-done | bytes 524320 | tf_op jit(solution)/shard_map/all_to_all | solution.py:126
  118.1 0.4 copy.99
  118.6 0.5 maximum_bitcast_fusion.1
  119.1 1.6 %reshape.15 = bf16[64,5120]{1,0:T(8,128)(2,1)} reshape(bf16[64,8,5,128]{3,2,1,0:T(8,128)(2,1)S(1)} %maximum_bitcast_fusion.1) | data formatting | bytes 1310720 | tf_op jit(solution)/shard_map/reshape | solution.py:136
  (24 shorter events, 0.6 us)
Async XLA Ops:
  0.0 2.4 %copy-start.6 = (bf16[64,5120]{1,0:T(8,128)(2,1)S(1)}, bf16[64,5120]{1,0:T(8,128)(2,1)}, u32[]{:S(2)}) copy-start(bf16[64,5120]{1,0:T(8,128)(2,1)} %param.4) | copy-start | bytes 1966084
  3.2 3.3 %copy-start.3 = (bf16[64,8,5,128]{3,2,1,0:T(8,128)(2,1)}, bf16[64,8,5,128]{3,2,1,0:T(8,128)(2,1)S(1)}, u32[]{:S(2)}) copy-start(bf16[64,8,5,128]{3,2,1,0:T(8,128)(2,1)S(1)} %reshape.13) | copy-start | bytes 1966084
  3.2 1.6 %copy-start.7 = (bf16[64,5120]{1,0:T(8,128)(2,1)S(1)}, bf16[64,5120]{1,0:T(8,128)(2,1)}, u32[]{:S(2)}) copy-start(bf16[64,5120]{1,0:T(8,128)(2,1)} %param.5) | copy-start | bytes 1966084
  6.5 1.7 %copy-start.5 = (bf16[1,64,16,2,128]{4,1,3,0,2:T(8,128)(2,1)S(1)}, bf16[1,64,16,2,128]{4,1,3,0,2:T(8,128)(2,1)}, u32[]{:S(2)}) copy-start(bf16[1,64,16,2,128]{4,1,3,0,2:T(8,128)(2,1)} %copy.88) | copy-start | bytes 1572868
  9.6 42.4 %all-to-all-start = ((bf16[16,3,2,64,128]{4,3,2,1,0:T(8,128)(2,1)}), bf16[16,3,2,64,128]{4,3,2,1,0:T(8,128)(2,1)S(1)}, u32[]{:S(2)}, u32[]{:S(2)}) async-start(bf16[16,3,2,64,128]{4,3,2,1,0:T(8,128)(2,1)} %maximum_bitcast_fusion), calls=%async_computation | async-start | bytes 3145728 | tf_op jit(solution)/shard_map/all_to_all | solution.py:104
  52.0 27.5 %copy-start = (bf16[16,3,2,64,128]{4,3,2,1,0:T(8,128)(2,1)}, bf16[16,3,2,64,128]{4,3,2,1,0:T(8,128)(2,1)S(1)}, u32[]{:S(2)}) copy-start(bf16[16,3,2,64,128]{4,3,2,1,0:T(8,128)(2,1)S(1)} %all-to-all-done.refs_0_.refs_1_.refs_2_) | copy-start | bytes 4718596
  52.0 18.1 %all-to-all-start.2 = ((bf16[8,3,1,64,128]{4,3,1,2,0:T(8,128)(2,1)}), bf16[8,3,1,64,128]{4,3,1,2,0:T(8,128)(2,1)S(1)}, u32[]{:S(2)}, u32[]{:S(2)}) async-start(bf16[8,3,1,64,128]{4,3,1,2,0:T(8,128)(2,1)} %copy.90), calls=%async_computation.2 | async-start | bytes 786432 | tf_op jit(solution)/shard_map/all_to_all | solution.py:108
  59.5 28.4 %collective-permute-start = (bf16[16,3,2,64,128]{4,3,2,1,0:T(8,128)(2,1)S(1)}, bf16[16,3,2,64,128]{4,3,2,1,0:T(8,128)(2,1)S(1)}, u32[]{:S(2)}, u32[]{:S(2)}) collective-permute-start(bf16[16,3,2,64,128]{4,3,2,1,0:T(8,128)(2,1)S(1)} %all-to-all-done.refs_0_.refs_1_.refs_2_), channel_id=1, source_target_pairs={{0,1},{1,0},{2,3},{3,2},{4,5},{5,4},{6,7},{7,6},{8,9},{9,8},{10,11... | collective-permute-start | bytes 4718600 | tf_op jit(solution)/shard_map/ppermute | solution.py:17
  70.1 9.4 %copy-start.1 = (bf16[8,3,1,64,128]{4,3,1,2,0:T(8,128)(2,1)}, bf16[8,3,1,64,128]{4,3,1,2,0:T(8,128)(2,1)S(1)}, u32[]{:S(2)}) copy-start(bf16[8,3,1,64,128]{4,3,1,2,0:T(8,128)(2,1)S(1)} %all-to-all-done.2) | copy-start | bytes 1179652
  70.2 6.4 %collective-permute-start.1 = (bf16[8,2,1,64,128]{4,3,1,0,2:T(8,128)(2,1)S(1)}, bf16[8,2,1,64,128]{4,3,1,0,2:T(8,128)(2,1)S(1)}, u32[]{:S(2)}, u32[]{:S(2)}) collective-permute-start(bf16[8,2,1,64,128]{4,3,1,0,2:T(8,128)(2,1)S(1)} %get-tuple-element.8), channel_id=1, source_target_pairs={{0,2},{2,0},{4,6},{6,4},{8,10},{10,8},{12,14},{14,12},{16,18},{18,... | collective-permute-start | bytes 786440 | tf_op jit(solution)/shard_map/ppermute | solution.py:122
  76.7 2.9 %copy-start.4 = (bf16[8,2,1,64,128]{4,3,1,0,2:T(8,128)(2,1)}, bf16[8,2,1,64,128]{4,3,1,0,2:T(8,128)(2,1)S(1)}, u32[]{:S(2)}) copy-start(bf16[8,2,1,64,128]{4,3,1,0,2:T(8,128)(2,1)S(1)} %collective-permute-done.1) | copy-start | bytes 786436
  76.7 2.0 %collective-permute-start.2 = (bf16[2,8,2,1,64,128]{5,4,2,1,3,0:T(8,128)(2,1)S(1)}, bf16[2,8,2,1,64,128]{5,4,2,1,3,0:T(8,128)(2,1)S(1)}, u32[]{:S(2)}, u32[]{:S(2)}) collective-permute-start(bf16[2,8,2,1,64,128]{5,4,2,1,3,0:T(8,128)(2,1)S(1)} %pad_maximum_fusion), channel_id=1, source_target_pairs={{0,1},{1,0},{2,3},{3,2},{4,5},{5,4},{6,7},{7,6},{8,9},{9,8},{10,11... | collective-permute-start | bytes 1572872 | tf_op jit(solution)/shard_map/ppermute | solution.py:17
  83.2 13.6 %all-to-all-start.3 = ((bf16[8,1,64,128]{3,2,1,0:T(8,128)(2,1)}), bf16[8,1,64,128]{3,2,1,0:T(8,128)(2,1)S(1)}, u32[]{:S(2)}, u32[]{:S(2)}) async-start(bf16[8,1,64,128]{3,2,1,0:T(8,128)(2,1)} %shard_map.38), calls=%async_computation.3 | async-start | bytes 262144 | tf_op jit(solution)/shard_map/all_to_all | solution.py:131
  88.0 1.1 copy-start.2
  96.8 21.3 %all-to-all-start.1 = ((bf16[16,2,64,128]{3,2,1,0:T(8,128)(2,1)}), bf16[16,2,64,128]{3,2,1,0:T(8,128)(2,1)S(1)}, u32[]{:S(2)}, u32[]{:S(2)}) async-start(bf16[16,2,64,128]{3,2,1,0:T(8,128)(2,1)} %shard_map.37), calls=%async_computation.1 | async-start | bytes 1048576 | tf_op jit(solution)/shard_map/all_to_all | solution.py:126
